TPU v7x, 256 devices: a whole 4x4x8 slice. The times are simulated.
256 devices in a mesh: expert: 16 (over z, core), shard: 16 (over y, x).
Axes of the slice: x: 4, y: 4, z: 8, core: 2. Of those that a mesh axis runs over, the one named last changes fastest.
Arguments:
- w_down: float32 [64, 1024, 2048], P('expert', None, 'shard'), may hold values from -0.25 to 0.25
- avg_down: float32 [64, 1024, 2048], P('expert', None, 'shard'), may hold values from -0.1875 to 0.1875
- mix_share: float32 [64], P('expert'), may hold values from 0.2 to 0.8
- router_weight: float32 [2048, 64], P('shard', 'expert'), may hold values from -0.125 to 0.125
- router_gain: float32 [2048], P('shard'), may hold values from 0.25 to 1.75
Outputs:
- serve_down: bfloat16 [64, 1024, 2048], P('expert')
- scale_down: float32 [64, 1024], P('expert')
- serve_router: bfloat16 [2048, 64], replicated
All inputs are finite; a program needn't handle non-finite values. Where the computation divides by a largest or mean magnitude, that divisor is 1e-20 or more.
Results may differ from a plain program's by a relative error of at most 0.001.
Values may be sent and summed in bfloat16 or wider, within the bound.
No kernel may reach another device: no remote copies, remote signals or barrier semaphores. Data moves between devices by JAX's collectives and lax.ppermute only.
A program may use at most 128 MiB of HBM per device.

v0:
```python
import jax
import jax.numpy as jnp
from jax import lax
from jax.sharding import PartitionSpec as P

D_MODEL = 2048


def sent_to_all(value, axis):
    copies = jnp.broadcast_to(value, (lax.axis_size(axis), *value.shape))
    return lax.all_to_all(copies, axis, split_axis=0, concat_axis=0, tiled=True)


def taken_together(value, axis):
    everything = sent_to_all(value, axis)
    return jnp.sum(everything, axis=0)


def laid_out(tiles, dim):
    shape = list(tiles.shape[1:])
    shape[dim] *= tiles.shape[0]
    return jnp.moveaxis(tiles, 0, dim).reshape(shape)


def gathered_copies(value, axis, dim):
    return laid_out(sent_to_all(value, axis), dim)


def body(w_down, avg_down, mix_share, router_weight, router_gain):
    fresh_down = mix_share[:, None, None] * w_down + (1.0 - mix_share[:, None, None]) * avg_down
    total_down = taken_together(jnp.sum(jnp.abs(fresh_down), axis=2), "shard")
    scale_down = total_down / D_MODEL
    narrow_down = (fresh_down / jnp.expand_dims(scale_down, 2)).astype(jnp.bfloat16)
    serve_down = lax.all_gather(narrow_down, "shard", axis=2, tiled=True)
    part_router = (router_weight * router_gain[:, None]).astype(jnp.bfloat16)
    row_router = gathered_copies(part_router, "shard", 0)
    serve_router = lax.all_gather(row_router, "expert", axis=1, tiled=True)
    return (serve_down, scale_down, serve_router)


def solution(mesh):
    return jax.shard_map(
        body,
        mesh=mesh,
        in_specs=(
            P("expert", None, "shard"),
            P("expert", None, "shard"),
            P("expert"),
            P("shard", "expert"),
            P("shard"),
        ),
        out_specs=(P("expert", None, None), P("expert", None), P()),
        check_vma=False,
    )
```

profile of v0, /device:TPU:2, one launch (start us, length us, event | category | flops | bytes accessed | tf_op | source)
XLA Modules:
  0.0 174.2 jit_solution(17278753643345742411)
XLA Ops:
  7.2 0.0 all-gather.3.cloned.1.call-start
  7.2 0.7 broadcast_subtract_fusion
  7.9 0.0 copy-start
  7.9 0.0 copy-start.2
  7.9 3.1 %abs_reduce_fusion = f32[4,1024]{1,0:T(4,128)S(1)} fusion(f32[4,1024,128]{2,1,0:T(8,128)} %param.6, f32[4]{0:T(128)S(1)} %broadcast_subtract_fusion, f32[4,1024,128]{2,1,0:T(8,128)} %param.5, f32[4]{0:T(128)} %param.7), kind=kLoop, calls=%fused_computation.1 | loop fusion | flops 2617344 | bytes 4210720 | tf_op jit(solution)/shard_map/reduce_sum | solution.py:31
  11.0 14.6 %all_to_all.10 = f32[16,4,1024]{2,1,0:T(4,128)S(1)} all-to-all(f32[16,4,1024]{2,1,0:T(4,128)S(1)} %broadcast_in_dim.4), channel_id=1, replica_groups=mesh['expert'=16,'shard'=16] {'shard'}, dimensions={0} | all-to-all | bytes 524288 | tf_op jit(solution)/shard_map/all_to_all | solution.py:11
  25.6 0.1 reduce_sum.19
  25.7 0.0 copy-done
  25.7 0.0 copy-done.2
  25.7 0.0 copy-start.1
  25.7 0.0 copy-start.3
  25.7 0.0 copy-start.4
  25.7 2.8 %divide_convert_fusion = bf16[4,1024,128]{2,1,0:T(8,128)(2,1)} fusion(f32[4,1024]{1,0:T(4,128)S(1)} %broadcast_multiply_fusion, f32[4,1024,128]{2,1,0:T(8,128)S(1)} %copy-done, f32[4]{0:T(128)S(1)} %broadcast_subtract_fusion, f32[4,1024,128]{2,1,0:T(8,128)} %param.5, f32[4]{0:T(128)S(1)} %copy-done.2), kind=kLoop, calls=%fused_computation | loop fusion | flops 2621440 | bytes 5259296 | tf_op jit(solution)/shard_map/convert_element_type | solution.py:33
  28.5 0.0 copy-done.1
  28.5 0.0 all-gather.3.cloned.1.call-update
  28.5 0.0 copy-done.3
  28.5 0.0 copy-done.4
  28.6 10.5 %all_to_all.11 = bf16[16,128,4]{1,2,0:T(4,128)(2,1)S(1)} all-to-all(bf16[16,128,4]{1,2,0:T(4,128)(2,1)S(1)} %broadcast_in_dim.5), channel_id=1, replica_groups=mesh['expert'=16,'shard'=16] {'shard'}, dimensions={0} | all-to-all | bytes 32768 | tf_op jit(solution)/shard_map/all_to_all | solution.py:11
  39.1 20.7 %all-gather = bf16[16,4,2048]{2,1,0:T(4,128)(2,1)S(1)} all-gather(bf16[1,4,2048]{2,1,0:T(4,128)(2,1)S(1)} %bitcast.7), channel_id=1, replica_groups=mesh['expert'=16,'shard'=16] {'expert'}, dimensions={0}, use_global_device_ids=true | all-gather | bytes 278528 | tf_op jit(solution)/shard_map/all_gather | solution.py:37
  59.7 0.8 reshape.18
  60.5 92.7 %all-gather.3.cloned.1.call-done = bf16[4,1024,2048]{2,1,0:T(8,128)(2,1)} async-done(((bf16[4,1024,128]{2,1,0:T(8,128)(2,1)}), bf16[4,1024,2048]{2,1,0:T(8,128)(2,1)}) %all-gather.3.cloned.1.call-update) | async-done | bytes 16777232 | tf_op jit(solution)/shard_map/all_gather | solution.py:34
  153.2 14.2 %copy.11 = bf16[4,1024,2048]{2,1,0:T(8,128)(2,1)} copy(bf16[4,1024,2048]{2,1,0:T(8,128)(2,1)} %all-gather.3.cloned.1.call-done) | data formatting | bytes 33554432
  (4 shorter events, 0.1 us)
Async XLA Ops:
  7.2 146.0 %all-gather.3.cloned.1.call-start = ((), (), s32[]{:S(2)}) async-start(), calls=%async_computation.2 | async-start | bytes 17825792 | tf_op jit(solution)/shard_map/all_gather | solution.py:34
  7.9 17.8 %copy-start = (f32[4,1024,128]{2,1,0:T(8,128)S(1)}, f32[4,1024,128]{2,1,0:T(8,128)}, u32[]{:S(2)}) copy-start(f32[4,1024,128]{2,1,0:T(8,128)} %param.6) | copy-start | bytes 6291460
  7.9 17.8 %copy-start.2 = (f32[4]{0:T(128)S(1)}, f32[4]{0:T(128)}, u32[]{:S(2)}) copy-start(f32[4]{0:T(128)} %param.7) | copy-start | bytes 52
  25.7 2.8 %copy-start.1 = (f32[4,1024]{1,0:T(4,128)}, f32[4,1024]{1,0:T(4,128)S(1)}, u32[]{:S(2)}) copy-start(f32[4,1024]{1,0:T(4,128)S(1)} %broadcast_multiply_fusion) | copy-start | bytes 49156
  25.7 2.8 %copy-start.3 = (f32[128,4]{0,1:T(4,128)S(1)}, f32[128,4]{0,1:T(4,128)}, u32[]{:S(2)}) copy-start(f32[128,4]{0,1:T(4,128)} %param.8) | copy-start | bytes 6148
  25.7 2.8 %copy-start.4 = (f32[128]{0:T(128)S(1)}, f32[128]{0:T(128)}, u32[]{:S(2)}) copy-start(f32[128]{0:T(128)} %param.9) | copy-start | bytes 1540
Sparse Core Ops, SparseCore 0:
  28.6 124.4 all-gather.2
where the time goes:
time: 174 us
  waiting for transfers between devices  92.7 us (53%)
  blocking collectives  45.8 us (26%)
  local copies, waits for them, and re-layouts  15 us (9%)
  between operations  14.1 us (8%)
  other arithmetic  6.58 us (4%)
    all_gather x1, waiting for transfers between devices, body(): serve_down = lax.all_gather(narrow_down, 'shard', axis=2, tiled=True)  92.7 us
    all_to_all x2, blocking collectives, sent_to_all(): return lax.all_to_all(copies, axis, split_axis=0, concat_axis=0, tiled=True)  25.1 us
    all_gather x1, blocking collectives, body(): serve_router = lax.all_gather(row_router, 'expert', axis=1, tiled=True)  20.7 us
    unnamed x12, local copies, waits for them, and re-layouts  14.9 us
  transfers between devices with their start and end apart: 1, of which 1 were waited for; matrix products, arithmetic and copies ran while one was open for 0% of the time, Pallas kernels for 0%

commit v1 on v0

--- a/solution.py
+++ b/solution.py
@@ -31,7 +31,8 @@
     total_down = taken_together(jnp.sum(jnp.abs(fresh_down), axis=2), "shard")
     scale_down = total_down / D_MODEL
     narrow_down = (fresh_down / jnp.expand_dims(scale_down, 2)).astype(jnp.bfloat16)
-    serve_down = lax.all_gather(narrow_down, "shard", axis=2, tiled=True)
+    make_slot = lambda here_x: jnp.concatenate(lax.all_gather(here_x, "shard"), axis=2)
+    serve_down = make_slot(narrow_down)
     part_router = (router_weight * router_gain[:, None]).astype(jnp.bfloat16)
     row_router = gathered_copies(part_router, "shard", 0)
     serve_router = lax.all_gather(row_router, "expert", axis=1, tiled=True)

time: 174 us -> 168 us (0.966)
  waiting for transfers between devices: 92.7 us -> 84.4 us
    reshape x0 -> x1, local copies, waits for them, and re-layouts: none -> 15.3 us  [body(): jnp.concatenate(lax.all_gather(here_x, 'shard'), axis=2)]
    unnamed x12 -> x11, local copies, waits for them, and re-layouts: 14.9 us -> 0.79 us
    all_gather x1, waiting for transfers between devices: 92.7 us -> 84.3 us  [body(): lax.all_gather(here_x, 'shard')]
where the time goes in v1:
time: 168 us; the launch traced here: 167 us
  waiting for transfers between devices  84.4 us (50%)
  blocking collectives  45.8 us (27%)
  local copies, waits for them, and re-layouts  16.2 us (10%)
  between operations  14.1 us (8%)
  other arithmetic  6.58 us (4%)
    all_gather x1, waiting for transfers between devices, body(): lax.all_gather(here_x, 'shard')  84.3 us
    all_to_all x2, blocking collectives, sent_to_all(): return lax.all_to_all(copies, axis, split_axis=0, concat_axis=0, tiled=True)  25.1 us
    all_gather x1, blocking collectives, body(): serve_router = lax.all_gather(row_router, 'expert', axis=1, tiled=True)  20.7 us
    reshape x1, local copies, waits for them, and re-layouts, body(): jnp.concatenate(lax.all_gather(here_x, 'shard'), axis=2)  15.3 us
  transfers between devices with their start and end apart: 1, of which 1 were waited for; matrix products, arithmetic and copies ran while one was open for 0% of the time, Pallas kernels for 0%

profile of v1, /device:TPU:2, one launch (start us, length us, event | category | flops | bytes accessed | tf_op | source)
XLA Modules:
  0.0 167.0 jit_solution(15638362901246118198)
XLA Ops:
  7.2 0.0 all-gather.4.cloned.1.call-start
  7.2 0.7 broadcast_subtract_fusion
  7.9 0.0 copy-start
  7.9 0.0 copy-start.2
  7.9 3.1 %abs_reduce_fusion = f32[4,1024]{1,0:T(4,128)S(1)} fusion(f32[4,1024,128]{2,1,0:T(8,128)} %param.6, f32[4]{0:T(128)S(1)} %broadcast_subtract_fusion, f32[4,1024,128]{2,1,0:T(8,128)} %param.5, f32[4]{0:T(128)} %param.7), kind=kLoop, calls=%fused_computation.2 | loop fusion | flops 2617344 | bytes 4210720 | tf_op jit(solution)/shard_map/reduce_sum | solution.py:31
  11.0 14.6 %all_to_all.10 = f32[16,4,1024]{2,1,0:T(4,128)S(1)} all-to-all(f32[16,4,1024]{2,1,0:T(4,128)S(1)} %broadcast_in_dim.4), channel_id=1, replica_groups=mesh['expert'=16,'shard'=16] {'shard'}, dimensions={0} | all-to-all | bytes 524288 | tf_op jit(solution)/shard_map/all_to_all | solution.py:11
  25.6 0.1 reduce_sum.19
  25.7 0.0 copy-done
  25.7 0.0 copy-done.2
  25.7 0.0 copy-start.1
  25.7 0.0 copy-start.3
  25.7 0.0 copy-start.4
  25.7 2.8 %divide_convert_fusion = bf16[4,1024,128]{2,1,0:T(8,128)(2,1)} fusion(f32[4,1024]{1,0:T(4,128)S(1)} %broadcast_multiply_fusion, f32[4,1024,128]{2,1,0:T(8,128)S(1)} %copy-done, f32[4]{0:T(128)S(1)} %broadcast_subtract_fusion, f32[4,1024,128]{2,1,0:T(8,128)} %param.5, f32[4]{0:T(128)S(1)} %copy-done.2), kind=kLoop, calls=%fused_computation.1 | loop fusion | flops 2621440 | bytes 5259296 | tf_op jit(solution)/shard_map/convert_element_type | solution.py:33
  28.5 0.0 copy-done.1
  28.5 0.0 all-gather.4.cloned.1.call-update
  28.5 0.0 copy-done.3
  28.5 0.0 copy-done.4
  28.6 10.5 %all_to_all.11 = bf16[16,128,4]{1,2,0:T(4,128)(2,1)S(1)} all-to-all(bf16[16,128,4]{1,2,0:T(4,128)(2,1)S(1)} %broadcast_in_dim.5), channel_id=1, replica_groups=mesh['expert'=16,'shard'=16] {'shard'}, dimensions={0} | all-to-all | bytes 32768 | tf_op jit(solution)/shard_map/all_to_all | solution.py:11
  39.1 20.7 %all-gather.1 = bf16[16,4,2048]{2,1,0:T(4,128)(2,1)S(1)} all-gather(bf16[1,4,2048]{2,1,0:T(4,128)(2,1)S(1)} %bitcast.16), channel_id=1, replica_groups=mesh['expert'=16,'shard'=16] {'expert'}, dimensions={0}, use_global_device_ids=true | all-gather | bytes 278528 | tf_op jit(solution)/shard_map/all_gather | solution.py:38
  59.7 0.8 reshape.27
  60.5 84.3 %all-gather.4.cloned.1.call-done = bf16[64,1024,128]{2,1,0:T(8,128)(2,1)} async-done(((bf16[4,1024,128]{2,1,0:T(8,128)(2,1)}), bf16[64,1024,128]{2,1,0:T(8,128)(2,1)}) %all-gather.4.cloned.1.call-update) | async-done | bytes 16777232 | tf_op jit(solution)/shard_map/all_gather | solution.py:34
  144.8 15.3 %copy.16 = bf16[16,4,128,8,128]{4,3,0,2,1:T(8,128)(2,1)} copy(bf16[16,4,128,8,128]{4,3,2,1,0:T(8,128)(2,1)} %bitcast.13) | data formatting | bytes 33554432 | tf_op jit(solution)/shard_map/reshape | solution.py:34
  (4 shorter events, 0.1 us)
Async XLA Ops:
  7.2 137.7 %all-gather.4.cloned.1.call-start = ((), (), s32[]{:S(2)}) async-start(), calls=%async_computation.2 | async-start | bytes 17825792 | tf_op jit(solution)/shard_map/all_gather | solution.py:34
  7.9 17.8 %copy-start = (f32[4,1024,128]{2,1,0:T(8,128)S(1)}, f32[4,1024,128]{2,1,0:T(8,128)}, u32[]{:S(2)}) copy-start(f32[4,1024,128]{2,1,0:T(8,128)} %param.6) | copy-start | bytes 6291460
  7.9 17.8 %copy-start.2 = (f32[4]{0:T(128)S(1)}, f32[4]{0:T(128)}, u32[]{:S(2)}) copy-start(f32[4]{0:T(128)} %param.7) | copy-start | bytes 52
  25.7 2.8 %copy-start.1 = (f32[4,1024]{1,0:T(4,128)}, f32[4,1024]{1,0:T(4,128)S(1)}, u32[]{:S(2)}) copy-start(f32[4,1024]{1,0:T(4,128)S(1)} %broadcast_multiply_fusion) | copy-start | bytes 49156
  25.7 2.8 %copy-start.3 = (f32[128,4]{0,1:T(4,128)S(1)}, f32[128,4]{0,1:T(4,128)}, u32[]{:S(2)}) copy-start(f32[128,4]{0,1:T(4,128)} %param.8) | copy-start | bytes 6148
  25.7 2.8 %copy-start.4 = (f32[128]{0:T(128)S(1)}, f32[128]{0:T(128)}, u32[]{:S(2)}) copy-start(f32[128]{0:T(128)} %param.9) | copy-start | bytes 1540
Sparse Core Ops, SparseCore 0:
  28.6 116.1 all-gather.3
